TPU v7x, 32 devices: a whole 2x2x4 slice. The times are simulated.
32 devices in a mesh: shard: 4 (over y, x), ctx: 2 (over core), tp: 4 (over z).
Axes of the slice: x: 2, y: 2, z: 4, core: 2. Of those that a mesh axis runs over, the one named last changes fastest.
Arguments:
- tokens: bfloat16 [4, 2048, 2048], P('shard', 'ctx'), may hold values from -6 to 6
- lengths: int32 [4], P('shard'), may hold values from 512 to 2048, as said below
- cotangent: bfloat16 [4, 2048, 2048], P('shard', 'ctx'), may hold values from -6 to 6
- w_query: float32 [2048, 2048], P(('shard', 'ctx'), 'tp'), may hold values from -0.1875 to 0.1875
- w_key: float32 [2048, 2048], P(('shard', 'ctx'), 'tp'), may hold values from -0.1875 to 0.1875
- w_value: float32 [2048, 2048], P(('shard', 'ctx'), 'tp'), may hold values from -0.125 to 0.125
- w_output: float32 [2048, 2048], P('tp', ('shard', 'ctx')), may hold values from -1 to 1
- w_gate: float32 [2048, 8192], P(('shard', 'ctx'), 'tp'), may hold values from -0.125 to 0.125
- w_up: float32 [2048, 8192], P(('shard', 'ctx'), 'tp'), may hold values from -0.125 to 0.125
- w_down: float32 [8192, 2048], P('tp', ('shard', 'ctx')), may hold values from -0.0625 to 0.0625
Outputs:
- output: bfloat16 [4, 2048, 2048], P('shard', 'ctx')
- grad_tokens: float32 [4, 2048, 2048], P('shard', 'ctx')
- grad_query: float32 [2048, 2048], P(('shard', 'ctx'), 'tp')
- grad_key: float32 [2048, 2048], P(('shard', 'ctx'), 'tp')
- grad_value: float32 [2048, 2048], P(('shard', 'ctx'), 'tp')
- grad_output: float32 [2048, 2048], P('tp', ('shard', 'ctx'))
- grad_gate: float32 [2048, 8192], P(('shard', 'ctx'), 'tp')
- grad_up: float32 [2048, 8192], P(('shard', 'ctx'), 'tp')
- grad_down: float32 [8192, 2048], P('tp', ('shard', 'ctx'))
Inputs may be any that keep to these rules, and one draw needn't show every extreme that they name: Slots 0 to lengths[b] - 1 of sequence b are valid, the rest padding; some sequence is full and some has 512 valid slots.
All inputs are finite; a program needn't handle non-finite values.
Results may differ from a plain program's by a relative error of at most 0.014.
The roundings to bfloat16 on the way count: a program that leaves them out, or rounds other values in their place, can miss the bound.
Values may be sent and summed in bfloat16 or wider, within the bound.
A program may use at most 256 MiB of HBM per device.

v0:
```python
import jax
import jax.numpy as jnp
from jax import lax
from jax.sharding import PartitionSpec as P

HEAD_DIM = 128
EPSILON = 1e-05


def normalize(values):
    center = values - jnp.mean(values, axis=-1, keepdims=True)
    inv_scale = lax.rsqrt(jnp.mean(center * center, axis=-1, keepdims=True) + EPSILON)
    return (center * inv_scale, inv_scale)


def norm_back(normed, inv_scale, upstream):
    first_mean = jnp.mean(upstream, axis=-1, keepdims=True)
    second_mean = jnp.mean(upstream * normed, axis=-1, keepdims=True)
    return inv_scale * (upstream - first_mean - normed * second_mean)


def rope_tables(row_count, head_size, offset):
    positions = (jnp.arange(row_count) + offset).astype(jnp.float32)
    inverse = 10000.0 ** (-(jnp.arange(head_size // 2).astype(jnp.float32) * 2.0) / head_size)
    angles = positions[:, None] * inverse[None, :]
    angles = jnp.concatenate([angles, angles], axis=-1)
    return (jnp.cos(angles)[:, None, :], jnp.sin(angles)[:, None, :])


def turn_half(values):
    half_dim = values.shape[-1] // 2
    return jnp.concatenate([-values[..., half_dim:], values[..., :half_dim]], axis=-1)


def rotate(values, cosine, sine_table):
    return values * cosine + turn_half(values) * sine_table


def rotate_back(values, cosine, sine_table):
    return values * cosine - turn_half(values) * sine_table


def score_block(query_rows, keys_seq, length, row_start):
    block_rows = query_rows.shape[0]
    key_pos = jnp.arange(keys_seq.shape[0])
    row_pos = row_start + jnp.arange(block_rows)
    scores = jnp.einsum(
        "qhd,khd->hqk", query_rows, keys_seq, preferred_element_type=jnp.float32
    ) * HEAD_DIM ** (-0.5)
    allowed = (key_pos[None, :] <= row_pos[:, None]) & (key_pos[None, :] < length)
    return jnp.where(allowed[None], scores, -1e30)


def attend_forward(queries_seq, keys_seq, values_seq, length, offset):
    half_len, head_count, head_size = queries_seq.shape
    block_rows = min(512, half_len)
    block_count = half_len // block_rows
    grouped = queries_seq.reshape(block_count, block_rows, head_count, head_size)

    def one_block(paired):
        query_rows, block_index = paired
        scores = score_block(query_rows, keys_seq, length, offset + block_index * block_rows)
        row_peak = jnp.max(scores, axis=-1, keepdims=True)
        log_total = jnp.log(jnp.sum(jnp.exp(scores - row_peak), axis=-1, keepdims=True)) + row_peak
        probability = jnp.exp(scores - log_total).astype(jnp.bfloat16)
        attended = jnp.einsum(
            "hqk,khd->qhd", probability, values_seq, preferred_element_type=jnp.float32
        )
        return (attended.astype(jnp.bfloat16), log_total[..., 0])

    attended, log_totals = lax.map(one_block, (grouped, jnp.arange(block_count)))
    return (attended.reshape(half_len, head_count, head_size), log_totals)


def attend_backward(queries_seq, keys_seq, values_seq, length, offset, log_totals, grad_seq):
    half_len, head_count, head_size = queries_seq.shape
    block_rows = min(512, half_len)
    block_count = half_len // block_rows
    score_scale = HEAD_DIM ** (-0.5)
    grouped = queries_seq.reshape(block_count, block_rows, head_count, head_size)
    grad_grouped = grad_seq.reshape(block_count, block_rows, head_count, head_size)

    def one_block(carried, paired):
        query_rows, grad_rows, log_rows, block_index = paired
        scores = score_block(query_rows, keys_seq, length, offset + block_index * block_rows)
        probability = jnp.exp(scores - log_rows[..., None])
        prob_low = probability.astype(jnp.bfloat16)
        grad_prob = jnp.einsum(
            "qhd,khd->hqk", grad_rows, values_seq, preferred_element_type=jnp.float32
        )
        inner_sum = jnp.sum(probability * grad_prob, axis=-1, keepdims=True)
        grad_scores = (probability * (grad_prob - inner_sum)).astype(jnp.bfloat16)
        grad_query_rows = (
            jnp.einsum("hqk,khd->qhd", grad_scores, keys_seq, preferred_element_type=jnp.float32)
            * score_scale
        )
        key_part = (
            jnp.einsum("hqk,qhd->khd", grad_scores, query_rows, preferred_element_type=jnp.float32)
            * score_scale
        )
        value_part = jnp.einsum(
            "hqk,qhd->khd", prob_low, grad_rows, preferred_element_type=jnp.float32
        )
        return ((carried[0] + key_part, carried[1] + value_part), grad_query_rows)

    empty = jnp.zeros(keys_seq.shape, jnp.float32)
    sums, grad_queries = lax.scan(
        one_block, (empty, empty), (grouped, grad_grouped, log_totals, jnp.arange(block_count))
    )
    return (grad_queries.reshape(half_len, head_count, head_size), sums[0], sums[1])


def scatter_low(grad, dim):
    summed = lax.psum_scatter(
        grad.astype(jnp.bfloat16), ("shard", "ctx"), scatter_dimension=dim, tiled=True
    )
    return summed.astype(jnp.float32)


def matmul_low(left, right):
    return jnp.dot(left, right, preferred_element_type=jnp.float32)


def body(tokens, lengths, cotangent, w_query, w_key, w_value, w_output, w_gate, w_up, w_down):
    seq_count, half_len, model_width = tokens.shape
    head_cols = w_query.shape[1]
    head_count = head_cols // HEAD_DIM
    row_total = seq_count * half_len
    offset = lax.axis_index("ctx") * half_len
    positions = offset + jnp.arange(half_len)
    valid_mask = (positions[None, :] < lengths[:, None]).astype(jnp.float32)
    bf_type = jnp.bfloat16
    attn_low = (
        w_query.astype(bf_type),
        w_key.astype(bf_type),
        w_value.astype(bf_type),
        w_output.astype(bf_type),
    )
    mlp_low = (w_gate.astype(bf_type), w_up.astype(bf_type), w_down.astype(bf_type))
    query_full, key_full, value_full, output_full = (
        lax.all_gather(attn_low[0], ("shard", "ctx"), axis=0, tiled=True),
        lax.all_gather(attn_low[1], ("shard", "ctx"), axis=0, tiled=True),
        lax.all_gather(attn_low[2], ("shard", "ctx"), axis=0, tiled=True),
        lax.all_gather(attn_low[3], ("shard", "ctx"), axis=1, tiled=True),
    )
    gate_full, up_full, down_full = (
        lax.all_gather(mlp_low[0], ("shard", "ctx"), axis=0, tiled=True),
        lax.all_gather(mlp_low[1], ("shard", "ctx"), axis=0, tiled=True),
        lax.all_gather(mlp_low[2], ("shard", "ctx"), axis=1, tiled=True),
    )
    tokens_wide = tokens.astype(jnp.float32).reshape(row_total, model_width)
    normed_one, scale_one = normalize(tokens_wide)
    input_one = normed_one.astype(bf_type)
    split_heads = (seq_count, half_len, head_count, HEAD_DIM)
    query_pre = matmul_low(input_one, query_full).reshape(split_heads)
    key_pre = matmul_low(input_one, key_full).reshape(split_heads)
    value_pre = matmul_low(input_one, value_full).reshape(split_heads)
    cosine, sine_table = rope_tables(half_len, HEAD_DIM, offset)
    queries = rotate(query_pre, cosine, sine_table).astype(bf_type)
    keys_rot = rotate(key_pre, cosine, sine_table).astype(bf_type)
    values_low = value_pre.astype(bf_type)
    keys_all, values_all = (
        lax.all_gather(keys_rot, "ctx", axis=1, tiled=True),
        lax.all_gather(values_low, "ctx", axis=1, tiled=True),
    )
    seq_index = 0
    attended, log_totals = attend_forward(
        queries[seq_index], keys_all[seq_index], values_all[seq_index], lengths[seq_index], offset
    )
    attended_list = [attended]
    log_list = [log_totals]
    attn_out = jnp.stack(attended_list).reshape(row_total, head_cols)
    branch_part = matmul_low(attn_out, output_full)
    resid = tokens_wide + lax.psum(branch_part.astype(bf_type), "tp").astype(jnp.float32)
    normed_two, scale_two = normalize(resid)
    input_two = normed_two.astype(bf_type)
    gate_proj = matmul_low(input_two, gate_full)
    up_proj = matmul_low(input_two, up_full)
    gate_sigmoid = jax.nn.sigmoid(gate_proj)
    hidden = (gate_proj * gate_sigmoid * up_proj).astype(bf_type)
    branch_two_part = matmul_low(hidden, down_full)
    final_sum = resid + lax.psum(branch_two_part.astype(jnp.bfloat16), "tp").astype(jnp.float32)
    grad_final = cotangent.astype(jnp.float32).reshape(row_total, model_width) * valid_mask.reshape(
        row_total, 1
    )
    grad_branch = grad_final.astype(bf_type)
    grad_down = jnp.einsum("rf,rd->fd", hidden, grad_branch, preferred_element_type=jnp.float32)
    grad_hidden = jnp.einsum(
        "rd,fd->rf", grad_branch, down_full, preferred_element_type=jnp.float32
    )
    grad_gate_act = (
        grad_hidden * up_proj * gate_sigmoid * (1.0 + gate_proj * (1.0 - gate_sigmoid))
    ).astype(bf_type)
    grad_up_act = (grad_hidden * gate_proj * gate_sigmoid).astype(bf_type)
    grad_gate = jnp.einsum(
        "rd,rf->df", input_two, grad_gate_act, preferred_element_type=jnp.float32
    )
    grad_up = jnp.einsum("rd,rf->df", input_two, grad_up_act, preferred_element_type=jnp.float32)
    grad_input_two = jnp.einsum(
        "rf,df->rd", grad_gate_act, gate_full, preferred_element_type=jnp.float32
    ) + jnp.einsum("rf,df->rd", grad_up_act, up_full, preferred_element_type=jnp.float32)
    mlp_grads = (scatter_low(grad_gate, 0), scatter_low(grad_up, 0), scatter_low(grad_down, 1))
    grad_input_two = lax.psum(grad_input_two.astype(bf_type), "tp").astype(jnp.float32)
    grad_resid = grad_final + norm_back(normed_two, scale_two, grad_input_two)
    grad_resid_low = grad_resid.astype(bf_type)
    grad_wout = jnp.einsum(
        "rc,rd->cd", attn_out, grad_resid_low, preferred_element_type=jnp.float32
    )
    grad_attn = jnp.einsum(
        "rd,cd->rc", grad_resid_low, output_full, preferred_element_type=jnp.float32
    )
    grad_attn = grad_attn.astype(bf_type).reshape(split_heads)
    seq_index = 0
    grad_queries, grad_keys_seq, grad_values_seq = attend_backward(
        queries[seq_index],
        keys_all[seq_index],
        values_all[seq_index],
        lengths[seq_index],
        offset,
        log_list[seq_index],
        grad_attn[seq_index],
    )
    query_grads = [grad_queries]
    key_grads = [grad_keys_seq]
    value_grads = [grad_values_seq]
    grad_keys, grad_values = (
        lax.psum_scatter(jnp.stack(key_grads), "ctx", scatter_dimension=1, tiled=True),
        lax.psum_scatter(jnp.stack(value_grads), "ctx", scatter_dimension=1, tiled=True),
    )
    grad_q_pre = (
        rotate_back(jnp.stack(query_grads), cosine, sine_table)
        .astype(bf_type)
        .reshape(row_total, head_cols)
    )
    grad_k_pre = (
        rotate_back(grad_keys, cosine, sine_table).astype(bf_type).reshape(row_total, head_cols)
    )
    grad_v_pre = grad_values.astype(bf_type).reshape(row_total, head_cols)
    grad_wq = jnp.einsum("rd,rc->dc", input_one, grad_q_pre, preferred_element_type=jnp.float32)
    grad_wk = jnp.einsum("rd,rc->dc", input_one, grad_k_pre, preferred_element_type=jnp.float32)
    grad_wv = jnp.einsum("rd,rc->dc", input_one, grad_v_pre, preferred_element_type=jnp.float32)
    grad_input_one = (
        jnp.einsum("rc,dc->rd", grad_q_pre, query_full, preferred_element_type=jnp.float32)
        + jnp.einsum("rc,dc->rd", grad_k_pre, key_full, preferred_element_type=jnp.float32)
        + jnp.einsum("rc,dc->rd", grad_v_pre, value_full, preferred_element_type=jnp.float32)
    )
    attn_grads = (
        scatter_low(grad_wq, 0),
        scatter_low(grad_wk, 0),
        scatter_low(grad_wv, 0),
        scatter_low(grad_wout, 1),
    )
    grad_input_one = lax.psum(grad_input_one.astype(bf_type), "tp").astype(jnp.float32)
    grad_tokens = grad_resid + norm_back(normed_one, scale_one, grad_input_one)
    output = final_sum.astype(bf_type).reshape(seq_count, half_len, model_width)
    grad_tokens = grad_tokens.reshape(seq_count, half_len, model_width)
    return (
        output,
        grad_tokens,
        attn_grads[0],
        attn_grads[1],
        attn_grads[2],
        attn_grads[3],
        mlp_grads[0],
        mlp_grads[1],
        mlp_grads[2],
    )


def solution(mesh):
    return jax.shard_map(
        body,
        mesh=mesh,
        in_specs=(
            P("shard", "ctx", None),
            P("shard"),
            P("shard", "ctx", None),
            P(("shard", "ctx"), "tp"),
            P(("shard", "ctx"), "tp"),
            P(("shard", "ctx"), "tp"),
            P("tp", ("shard", "ctx")),
            P(("shard", "ctx"), "tp"),
            P(("shard", "ctx"), "tp"),
            P("tp", ("shard", "ctx")),
        ),
        out_specs=(
            P("shard", "ctx", None),
            P("shard", "ctx", None),
            P(("shard", "ctx"), "tp"),
            P(("shard", "ctx"), "tp"),
            P(("shard", "ctx"), "tp"),
            P("tp", ("shard", "ctx")),
            P(("shard", "ctx"), "tp"),
            P(("shard", "ctx"), "tp"),
            P("tp", ("shard", "ctx")),
        ),
        check_vma=False,
    )
```

profile of v0, /device:TPU:0, one launch (start us, length us, event | category | flops | bytes accessed | tf_op | source)
XLA Modules:
  0.0 1603.9 jit_solution(9619642317359347338)
XLA Ops:
  21.9 19.1 %all-gather.13.cloned.1.call-done = bf16[2048,512]{1,0:T(8,128)(2,1)} async-done(((bf16[256,512]{1,0:T(8,128)(2,1)}), bf16[2048,512]{1,0:T(8,128)(2,1)}) %all-gather.13.cloned.1.call-update) | async-done | bytes 2097168 | tf_op jit(solution)/shard_map/all_gather | solution.py:142
  48.2 23.1 %all-gather.17.cloned.1.call-done = bf16[2048,512]{1,0:T(8,128)(2,1)} async-done(((bf16[256,512]{1,0:T(8,128)(2,1)}), bf16[2048,512]{1,0:T(8,128)(2,1)}) %all-gather.17.cloned.1.call-update) | async-done | bytes 2097168 | tf_op jit(solution)/shard_map/all_gather | solution.py:143
  84.3 17.2 %all-gather.11.cloned.1.call-done = bf16[2048,512]{1,0:T(8,128)(2,1)} async-done(((bf16[256,512]{1,0:T(8,128)(2,1)}), bf16[2048,512]{1,0:T(8,128)(2,1)}) %all-gather.11.cloned.1.call-update) | async-done | bytes 2097168 | tf_op jit(solution)/shard_map/all_gather | solution.py:141
  131.7 34.9 %while.27 = (s32[]{:T(128)}, bf16[2,512,4,128]{3,2,1,0:T(4,128)(2,1)}, f32[2,4,512]{2,1,0:T(4,128)S(1)}, s32[2]{0:T(128)S(1)}, s32[]{:T(128)}, /*index=5*/s32[]{...) while((s32[]{:T(128)}, ...), condition=%wide.region_5.6_spmd, body=%wide.region_2.5_spmd.sunk | while | flops 2195980800 | bytes 77668600 | solution.py:71
  182.3 146.1 %all-reduce.5.cloned.1.call-done = bf16[1024,2048]{1,0:T(8,128)(2,1)} async-done(((bf16[1024,2048]{1,0:T(8,128)(2,1)}), bf16[1024,2048]{1,0:T(8,128)(2,1)}) %all-reduce.5.cloned.1.call-update) | async-done | bytes 4194320 | tf_op jit(solution)/shard_map/psum | solution.py:174
  339.8 44.3 %all-gather.21.cloned.1.call-done = bf16[2048,2048]{1,0:T(8,128)(2,1)} async-done(((bf16[256,2048]{1,0:T(8,128)(2,1)}), bf16[2048,2048]{1,0:T(8,128)(2,1)}) %all-gather.21.cloned.1.call-update) | async-done | bytes 8388624 | tf_op jit(solution)/shard_map/all_gather | solution.py:147
  384.1 14.5 fusion.113
  398.6 42.3 %all-gather.23.cloned.1.call-done = bf16[2048,2048]{1,0:T(8,128)(2,1)} async-done(((bf16[256,2048]{1,0:T(8,128)(2,1)}), bf16[2048,2048]{1,0:T(8,128)(2,1)}) %all-gather.23.cloned.1.call-update) | async-done | bytes 8388624 | tf_op jit(solution)/shard_map/all_gather | solution.py:148
  440.9 14.5 fusion.114
  455.4 43.6 %all-gather.25.cloned.1.call-done = bf16[2048,2048]{1,0:T(8,128)(2,1)} async-done(((bf16[2048,256]{1,0:T(8,128)(2,1)}), bf16[2048,2048]{1,0:T(8,128)(2,1)}) %all-gather.25.cloned.1.call-update) | async-done | bytes 8388624 | tf_op jit(solution)/shard_map/all_gather | solution.py:149
  499.1 22.3 %multiply_convert_fusion.1 = (bf16[1024,2048]{1,0:T(8,128)(2,1)}, bf16[1024,2048]{1,0:T(8,128)(2,1)}, bf16[1024,2048]{1,0:T(8,128)(2,1)}) fusion(f32[1024,2048]{1,0:T(8,128)} %fusion.113, f32[1024,2048]{1,0:T(8,128)} %fusion.114, bf16[2048,2048]{1,0:T(8,128)(2,1)} %all-gather.25.cloned.1.call-done, bf16[1,1024,2048]{2,1,0:T(8,128)(2,1)} %param.16, ...), kind=kOutput, calls=%fused_computation.80 | convolution fusion | flops 8629780480 | bytes 41947136 | tf_op jit(solution)/shard_map/rd,fd->rf/dot_general | solution.py:188
  521.3 14.7 fusion.115
  548.3 155.1 %all-reduce.7.cloned.1.call-done = bf16[1024,2048]{1,0:T(8,128)(2,1)} async-done(((bf16[1024,2048]{1,0:T(8,128)(2,1)}), bf16[1024,2048]{1,0:T(8,128)(2,1)}) %all-reduce.7.cloned.1.call-update) | async-done | bytes 4194320 | tf_op jit(solution)/shard_map/psum | solution.py:203
  726.7 127.9 %while.28 = (s32[]{:T(128)}, f32[2048,4,128]{0,2,1:T(8,128)}, f32[2048,4,128]{0,2,1:T(8,128)}, f32[2,512,4,128]{3,1,2,0:T(8,128)}, bf16[2,512,4,128]{3,1,2,0:T(8...) while((s32[]{:T(128)}, f32[2048,4,128]{0,2,1:T(8,128)}, ...), condition=%wide.region_15.16_spmd.clone, body=%wide.region_13.15_spmd.clone.sunk | while | flops 5439226368 | bytes 211878384 | solution.py:107
  752.2 14.9 multiply_convert_fusion.5
  814.8 14.9 multiply_convert_fusion.5
  873.1 15.2 convolution_convert_fusion.2
  903.0 14.5 convolution_convert_fusion
  973.9 73.1 %reduce-scatter.22.cloned.1.call-done = bf16[256,2048]{1,0:T(8,128)(2,1)} async-done(((bf16[2048,2048]{1,0:T(8,128)(2,1)}), bf16[256,2048]{1,0:T(8,128)(2,1)}) %reduce-scatter.22.cloned.1.call-update) | async-done | bytes 1048592 | tf_op jit(solution)/shard_map/reduce_scatter | solution.py:114
  1049.8 72.1 %reduce-scatter.24.cloned.1.call-done = bf16[256,2048]{1,0:T(8,128)(2,1)} async-done(((bf16[2048,2048]{1,0:T(8,128)(2,1)}), bf16[256,2048]{1,0:T(8,128)(2,1)}) %reduce-scatter.24.cloned.1.call-update) | async-done | bytes 1048592 | tf_op jit(solution)/shard_map/reduce_scatter | solution.py:114
  1124.7 71.9 %reduce-scatter.26.cloned.1.call-done = bf16[2048,256]{1,0:T(8,128)(2,1)} async-done(((bf16[2048,2048]{1,0:T(8,128)(2,1)}), bf16[2048,256]{1,0:T(8,128)(2,1)}) %reduce-scatter.26.cloned.1.call-update) | async-done | bytes 1048592 | tf_op jit(solution)/shard_map/reduce_scatter | solution.py:114
  1199.2 41.7 %reduce-scatter.16.cloned.1.call-done = bf16[256,512]{1,0:T(8,128)(2,1)} async-done(((bf16[2048,512]{1,0:T(8,128)(2,1)}), bf16[256,512]{1,0:T(8,128)(2,1)}) %reduce-scatter.16.cloned.1.call-update) | async-done | bytes 262160 | tf_op jit(solution)/shard_map/reduce_scatter | solution.py:114
  1242.7 42.5 %reduce-scatter.18.cloned.1.call-done = bf16[256,512]{1,0:T(8,128)(2,1)} async-done(((bf16[2048,512]{1,0:T(8,128)(2,1)}), bf16[256,512]{1,0:T(8,128)(2,1)}) %reduce-scatter.18.cloned.1.call-update) | async-done | bytes 262160 | tf_op jit(solution)/shard_map/reduce_scatter | solution.py:114
  1287.0 292.3 %all-reduce.9.cloned.1.call-done = (bf16[1024,2048]{1,0:T(8,128)(2,1)}, bf16[1024,2048]{1,0:T(8,128)(2,1)}) async-done(((bf16[1024,2048]{1,0:T(8,128)(2,1)}, bf16[1024,2048]{1,0:T(8,128)(2,1)}), (bf16[1024,2048]{1,0:T(8,128)(2,1)}, bf16[1024,2048]{1,0:T(8,128)(2,1)})) %all-reduce.9.cloned.1.call-update) | async-done | bytes 8388624 | tf_op jit(solution)/shard_map/psum | solution.py:182
  (305 shorter events, 374.6 us)
Async XLA Ops:
  7.2 33.8 %all-gather.13.cloned.1.call-start = ((), (), s32[]{:S(2)}) async-start(), calls=%async_computation.10 | async-start | bytes 2359296 | tf_op jit(solution)/shard_map/all_gather | solution.py:142
  9.0 62.2 %all-gather.17.cloned.1.call-start = ((), (), s32[]{:S(2)}) async-start(), calls=%async_computation.12 | async-start | bytes 2359296 | tf_op jit(solution)/shard_map/all_gather | solution.py:143
  10.9 90.6 %all-gather.11.cloned.1.call-start = ((), (), s32[]{:S(2)}) async-start(), calls=%async_computation.9 | async-start | bytes 2359296 | tf_op jit(solution)/shard_map/all_gather | solution.py:141
  12.7 115.8 %all-gather.15.cloned.1.call-start = ((), (), s32[]{:S(2)}) async-start(), calls=%async_computation.11 | async-start | bytes 3145728 | tf_op jit(solution)/shard_map/all_gather | solution.py:163
  18.0 56.2 %copy-start.38 = (f32[1024]{0:T(1024)}, f32[1024]{0:T(1024)S(1)}, u32[]{:S(2)}) copy-start(f32[1024]{0:T(1024)S(1)} %broadcast_multiply_fusion.7) | copy-start | bytes 12292
  19.3 54.9 %copy-start.42 = (f32[1024]{0:T(1024)}, f32[1024]{0:T(1024)S(1)}, u32[]{:S(2)}) copy-start(f32[1024]{0:T(1024)S(1)} %add_rsqrt_fusion.1) | copy-start | bytes 12292
  48.1 83.5 %all-gather.27.cloned.1.call-start = ((), (), s32[]{:S(2)}) async-start(), calls=%async_computation.28 | async-start | bytes 3145728 | tf_op jit(solution)/shard_map/all_gather | solution.py:164
  79.8 86.7 %all-gather.19.cloned.1.call-start = ((), (), s32[]{:S(2)}) async-start(), calls=%async_computation.13 | async-start | bytes 2359296 | tf_op jit(solution)/shard_map/all_gather | solution.py:144
  80.7 247.7 %all-reduce.5.cloned.1.call-start = ((), (), s32[]{:S(2)}) async-start(), calls=%async_computation.14 | async-start | bytes 8388608 | tf_op jit(solution)/shard_map/psum | solution.py:174
  172.9 211.2 %all-gather.21.cloned.1.call-start = ((), (), s32[]{:S(2)}) async-start(), calls=%async_computation.15 | async-start | bytes 9437184 | tf_op jit(solution)/shard_map/all_gather | solution.py:147
  175.7 265.2 %all-gather.23.cloned.1.call-start = ((), (), s32[]{:S(2)}) async-start(), calls=%async_computation.16 | async-start | bytes 9437184 | tf_op jit(solution)/shard_map/all_gather | solution.py:148
  178.5 320.6 %all-gather.25.cloned.1.call-start = ((), (), s32[]{:S(2)}) async-start(), calls=%async_computation.17 | async-start | bytes 9437184 | tf_op jit(solution)/shard_map/all_gather | solution.py:149
  181.6 521.8 %all-reduce.7.cloned.1.call-start = ((), (), s32[]{:S(2)}) async-start(), calls=%async_computation.18 | async-start | bytes 8388608 | tf_op jit(solution)/shard_map/psum | solution.py:203
  182.3 529.4 %copy-start.44 = (f32[1024]{0:T(1024)}, f32[1024]{0:T(1024)S(1)}, u32[]{:S(2)}) copy-start(f32[1024]{0:T(1024)S(1)} %fusion.106) | copy-start | bytes 12292
  548.2 369.4 %reduce-scatter.10.cloned.1.call-start = ((), (), s32[]{:S(2)}) async-start(), calls=%async_computation.19 | async-start | bytes 6291456 | tf_op jit(solution)/shard_map/reduce_scatter | solution.py:227
  854.7 73.6 %reduce-scatter.12.cloned.1.call-start = ((), (), s32[]{:S(2)}) async-start(), calls=%async_computation.20 | async-start | bytes 6291456 | tf_op jit(solution)/shard_map/reduce_scatter | solution.py:228
  855.4 111.1 %reduce-scatter.14.cloned.1.call-start = ((), (), s32[]{:S(2)}) async-start(), calls=%async_computation.21 | async-start | bytes 2359296 | tf_op jit(solution)/shard_map/reduce_scatter | solution.py:114
  865.8 106.3 %reduce-scatter.20.cloned.1.call-start = ((), (), s32[]{:S(2)}) async-start(), calls=%async_computation.24 | async-start | bytes 2359296 | tf_op jit(solution)/shard_map/reduce_scatter | solution.py:114
  873.0 174.0 %reduce-scatter.22.cloned.1.call-start = ((), (), s32[]{:S(2)}) async-start(), calls=%async_computation.25 | async-start | bytes 9437184 | tf_op jit(solution)/shard_map/reduce_scatter | solution.py:114
  888.2 233.6 %reduce-scatter.24.cloned.1.call-start = ((), (), s32[]{:S(2)}) async-start(), calls=%async_computation.26 | async-start | bytes 9437184 | tf_op jit(solution)/shard_map/reduce_scatter | solution.py:114
  902.3 294.2 %reduce-scatter.26.cloned.1.call-start = ((), (), s32[]{:S(2)}) async-start(), calls=%async_computation.27 | async-start | bytes 9437184 | tf_op jit(solution)/shard_map/reduce_scatter | solution.py:114
  917.5 323.4 %reduce-scatter.16.cloned.1.call-start = ((), (), s32[]{:S(2)}) async-start(), calls=%async_computation.22 | async-start | bytes 2359296 | tf_op jit(solution)/shard_map/reduce_scatter | solution.py:114
  926.8 358.4 %reduce-scatter.18.cloned.1.call-start = ((), (), s32[]{:S(2)}) async-start(), calls=%async_computation.23 | async-start | bytes 2359296 | tf_op jit(solution)/shard_map/reduce_scatter | solution.py:114
  937.6 641.7 %all-reduce.9.cloned.1.call-start = ((), (), s32[]{:S(2)}) async-start(), calls=%async_computation.29 | async-start | bytes 16777216 | tf_op jit(solution)/shard_map/psum | solution.py:182
  (60 other events, 400.4 us)
Sparse Core Ops, SparseCore 0:
  10.4 30.4 all-gather.12
  43.4 27.7 all-gather.16
  73.7 27.7 all-gather.10
  103.5 10.5 all-gather.14
  115.5 11.7 all-gather.26
  129.0 29.2 all-gather.18
  173.0 155.3 all-reduce.4
  330.8 53.2 all-gather.20
  386.6 54.2 all-gather.22
  443.2 55.8 all-gather.24
  548.4 154.9 all-reduce.6
  854.8 10.8 reduce-scatter.9
  867.9 13.1 reduce-scatter.11
  884.9 42.3 reduce-scatter.13
  931.0 41.1 reduce-scatter.19
  975.5 71.4 reduce-scatter.21
  1050.3 71.5 reduce-scatter.23
  1125.2 71.2 reduce-scatter.25
  1199.8 41.0 reduce-scatter.15
  1244.1 41.0 reduce-scatter.17
  1288.4 290.8 all-reduce.8
where the time goes:
time: 1610 us; the launch traced here: 1600 us
  waiting for transfers between devices  1090 us (68%)
  matrix products  301 us (19%)
  other arithmetic  143 us (9%)
  local copies, waits for them, and re-layouts  49.4 us (3%)
  between operations  16.3 us (1%)
    reduce_scatter x7, waiting for transfers between devices, scatter_low(): lax.psum_scatter(grad.astype(jnp.bfloat16), ('shard', 'ctx'), scatter_dim...  305 us
    psum x1, waiting for transfers between devices, body(): lax.psum(branch_two_part.astype(jnp.bfloat16), 'tp').astype(jnp.float32)  292 us
    psum x1, waiting for transfers between devices, body(): lax.psum(grad_input_two.astype(bf_type), 'tp').astype(jnp.float32)  155 us
    psum x1, waiting for transfers between devices, body(): lax.psum(branch_part.astype(bf_type), 'tp').astype(jnp.float32)  146 us
    dot_general x7, matrix products, matmul_low(): return jnp.dot(left, right, preferred_element_type=jnp.float32)  67.1 us
    all_gather x1, waiting for transfers between devices, body(): lax.all_gather(mlp_low[0], ('shard', 'ctx'), axis=0, tiled=True)  44.3 us
    all_gather x1, waiting for transfers between devices, body(): lax.all_gather(mlp_low[2], ('shard', 'ctx'), axis=1, tiled=True)  43.6 us
    all_gather x1, waiting for transfers between devices, body(): lax.all_gather(mlp_low[1], ('shard', 'ctx'), axis=0, tiled=True)  42.3 us
  transfers between devices with their start and end apart: 21, of which 15 were waited for; matrix products, arithmetic and copies ran while one was open for 16% of the time, Pallas kernels for 0%

commit v1 on v0

--- a/solution.py
+++ b/solution.py
@@ -200,7 +200,9 @@
         "rf,df->rd", grad_gate_act, gate_full, preferred_element_type=jnp.float32
     ) + jnp.einsum("rf,df->rd", grad_up_act, up_full, preferred_element_type=jnp.float32)
     mlp_grads = (scatter_low(grad_gate, 0), scatter_low(grad_up, 0), scatter_low(grad_down, 1))
-    grad_input_two = lax.psum(grad_input_two.astype(bf_type), "tp").astype(jnp.float32)
+    grad_input_two = jnp.sum(lax.all_gather(grad_input_two.astype(bf_type), "tp"), axis=0).astype(
+        jnp.float32
+    )
     grad_resid = grad_final + norm_back(normed_two, scale_two, grad_input_two)
     grad_resid_low = grad_resid.astype(bf_type)
     grad_wout = jnp.einsum(

time: 1610 us -> 1750 us (1.087)
  waiting for transfers between devices: 1090 us -> 1220 us
    all_gather x0 -> x1, waiting for transfers between devices: none -> 287 us  [body(): lax.all_gather(grad_input_two.astype(bf_type), 'tp')]
    psum x1 -> x0, waiting for transfers between devices: 155 us -> none  [body(): lax.psum(grad_input_two.astype(bf_type), 'tp').astype(jnp.float32)]
  transfers between devices with their start and end apart: 21 -> 21, of which waited for: 15 -> 15; matrix products, arithmetic and copies ran while one was open for 16% -> 15% of each run, Pallas kernels for 0% -> 0%
where the time goes in v1:
time: 1750 us
  waiting for transfers between devices  1220 us (70%)
  matrix products  300 us (17%)
  other arithmetic  156 us (9%)
  local copies, waits for them, and re-layouts  49.6 us (3%)
    reduce_scatter x7, waiting for transfers between devices, scatter_low(): lax.psum_scatter(grad.astype(jnp.bfloat16), ('shard', 'ctx'), scatter_dim...  304 us
    psum x1, waiting for transfers between devices, body(): lax.psum(branch_two_part.astype(jnp.bfloat16), 'tp').astype(jnp.float32)  292 us
    all_gather x1, waiting for transfers between devices, body(): lax.all_gather(grad_input_two.astype(bf_type), 'tp')  287 us
    psum x1, waiting for transfers between devices, body(): lax.psum(branch_part.astype(bf_type), 'tp').astype(jnp.float32)  146 us
    dot_general x7, matrix products, matmul_low(): return jnp.dot(left, right, preferred_element_type=jnp.float32)  66.9 us
    all_gather x1, waiting for transfers between devices, body(): lax.all_gather(mlp_low[0], ('shard', 'ctx'), axis=0, tiled=True)  44.3 us
    all_gather x1, waiting for transfers between devices, body(): lax.all_gather(mlp_low[2], ('shard', 'ctx'), axis=1, tiled=True)  43.6 us
    all_gather x1, waiting for transfers between devices, body(): lax.all_gather(mlp_low[1], ('shard', 'ctx'), axis=0, tiled=True)  42.3 us
  transfers between devices with their start and end apart: 21, of which 15 were waited for; matrix products, arithmetic and copies ran while one was open for 15% of the time, Pallas kernels for 0%

profile of v1, /device:TPU:0, one launch (start us, length us, event | category | flops | bytes accessed | tf_op | source)
XLA Modules:
  0.0 1745.7 jit_solution(18435968540365722762)
XLA Ops:
  21.9 19.1 %all-gather.15.cloned.1.call-done = bf16[2048,512]{1,0:T(8,128)(2,1)} async-done(((bf16[256,512]{1,0:T(8,128)(2,1)}), bf16[2048,512]{1,0:T(8,128)(2,1)}) %all-gather.15.cloned.1.call-update) | async-done | bytes 2097168 | tf_op jit(solution)/shard_map/all_gather | solution.py:142
  48.2 23.1 %all-gather.19.cloned.1.call-done = bf16[2048,512]{1,0:T(8,128)(2,1)} async-done(((bf16[256,512]{1,0:T(8,128)(2,1)}), bf16[2048,512]{1,0:T(8,128)(2,1)}) %all-gather.19.cloned.1.call-update) | async-done | bytes 2097168 | tf_op jit(solution)/shard_map/all_gather | solution.py:143
  84.3 17.2 all-gather.13.cloned.1.call-done
  131.7 34.9 %while.27 = (s32[]{:T(128)}, bf16[2,512,4,128]{3,2,1,0:T(4,128)(2,1)}, f32[2,4,512]{2,1,0:T(4,128)S(1)}, s32[2]{0:T(128)S(1)}, s32[]{:T(128)}, /*index=5*/s32[]{...) while((s32[]{:T(128)}, ...), condition=%wide.region_5.6_spmd, body=%wide.region_2.5_spmd.sunk | while | flops 2195980800 | bytes 77668600 | solution.py:71
  182.3 146.1 %all-reduce.4.cloned.1.call-done = bf16[1024,2048]{1,0:T(8,128)(2,1)} async-done(((bf16[1024,2048]{1,0:T(8,128)(2,1)}), bf16[1024,2048]{1,0:T(8,128)(2,1)}) %all-reduce.4.cloned.1.call-update) | async-done | bytes 4194320 | tf_op jit(solution)/shard_map/psum | solution.py:174
  339.8 44.3 %all-gather.23.cloned.1.call-done = bf16[2048,2048]{1,0:T(8,128)(2,1)} async-done(((bf16[256,2048]{1,0:T(8,128)(2,1)}), bf16[2048,2048]{1,0:T(8,128)(2,1)}) %all-gather.23.cloned.1.call-update) | async-done | bytes 8388624 | tf_op jit(solution)/shard_map/all_gather | solution.py:147
  384.1 14.5 fusion.113
  398.6 42.3 %all-gather.25.cloned.1.call-done = bf16[2048,2048]{1,0:T(8,128)(2,1)} async-done(((bf16[256,2048]{1,0:T(8,128)(2,1)}), bf16[2048,2048]{1,0:T(8,128)(2,1)}) %all-gather.25.cloned.1.call-update) | async-done | bytes 8388624 | tf_op jit(solution)/shard_map/all_gather | solution.py:148
  440.9 14.5 fusion.114
  455.4 43.6 %all-gather.27.cloned.1.call-done = bf16[2048,2048]{1,0:T(8,128)(2,1)} async-done(((bf16[2048,256]{1,0:T(8,128)(2,1)}), bf16[2048,2048]{1,0:T(8,128)(2,1)}) %all-gather.27.cloned.1.call-update) | async-done | bytes 8388624 | tf_op jit(solution)/shard_map/all_gather | solution.py:149
  499.1 22.3 %multiply_convert_fusion.1 = (bf16[1024,2048]{1,0:T(8,128)(2,1)}, bf16[1024,2048]{1,0:T(8,128)(2,1)}, bf16[1024,2048]{1,0:T(8,128)(2,1)}) fusion(f32[1024,2048]{1,0:T(8,128)} %fusion.113, f32[1024,2048]{1,0:T(8,128)} %fusion.114, bf16[2048,2048]{1,0:T(8,128)(2,1)} %all-gather.27.cloned.1.call-done, bf16[1,1024,2048]{2,1,0:T(8,128)(2,1)} %param.16, ...), kind=kOutput, calls=%fused_computation.80 | convolution fusion | flops 8629780480 | bytes 41947136 | tf_op jit(solution)/shard_map/rd,fd->rf/dot_general | solution.py:188
  521.3 14.7 fusion.115
  548.3 286.8 %all-gather.31.cloned.1.call-done = bf16[4096,2048]{1,0:T(8,128)(2,1)} async-done(((bf16[1024,2048]{1,0:T(8,128)(2,1)}), bf16[4096,2048]{1,0:T(8,128)(2,1)}) %all-gather.31.cloned.1.call-update) | async-done | bytes 16777232 | tf_op jit(solution)/shard_map/all_gather | solution.py:203
  870.9 127.9 %while.28 = (s32[]{:T(128)}, f32[2048,4,128]{0,2,1:T(8,128)}, f32[2048,4,128]{0,2,1:T(8,128)}, f32[2,512,4,128]{3,1,2,0:T(8,128)}, bf16[2,512,4,128]{3,1,2,0:T(8...) while((s32[]{:T(128)}, f32[2048,4,128]{0,2,1:T(8,128)}, ...), condition=%wide.region_15.16_spmd.clone, body=%wide.region_13.15_spmd.clone.sunk | while | flops 5439226368 | bytes 211878384 | solution.py:107
  896.2 14.9 multiply_convert_fusion.5
  958.8 14.9 multiply_convert_fusion.5
  1028.5 14.7 convolution_convert_fusion
  1112.8 62.7 %reduce-scatter.24.cloned.1.call-done = bf16[256,2048]{1,0:T(8,128)(2,1)} async-done(((bf16[2048,2048]{1,0:T(8,128)(2,1)}), bf16[256,2048]{1,0:T(8,128)(2,1)}) %reduce-scatter.24.cloned.1.call-update) | async-done | bytes 1048592 | tf_op jit(solution)/shard_map/reduce_scatter | solution.py:114
  1178.3 71.9 %reduce-scatter.26.cloned.1.call-done = bf16[2048,256]{1,0:T(8,128)(2,1)} async-done(((bf16[2048,2048]{1,0:T(8,128)(2,1)}), bf16[2048,256]{1,0:T(8,128)(2,1)}) %reduce-scatter.26.cloned.1.call-update) | async-done | bytes 1048592 | tf_op jit(solution)/shard_map/reduce_scatter | solution.py:114
  1252.9 41.6 %reduce-scatter.14.cloned.1.call-done = bf16[256,512]{1,0:T(8,128)(2,1)} async-done(((bf16[2048,512]{1,0:T(8,128)(2,1)}), bf16[256,512]{1,0:T(8,128)(2,1)}) %reduce-scatter.14.cloned.1.call-update) | async-done | bytes 262160 | tf_op jit(solution)/shard_map/reduce_scatter | solution.py:114
  1296.2 42.5 %reduce-scatter.20.cloned.1.call-done = bf16[512,256]{1,0:T(8,128)(2,1)} async-done(((bf16[512,2048]{1,0:T(8,128)(2,1)}), bf16[512,256]{1,0:T(8,128)(2,1)}) %reduce-scatter.20.cloned.1.call-update) | async-done | bytes 262160 | tf_op jit(solution)/shard_map/reduce_scatter | solution.py:114
  1340.5 42.7 %reduce-scatter.16.cloned.1.call-done = bf16[256,512]{1,0:T(8,128)(2,1)} async-done(((bf16[2048,512]{1,0:T(8,128)(2,1)}), bf16[256,512]{1,0:T(8,128)(2,1)}) %reduce-scatter.16.cloned.1.call-update) | async-done | bytes 262160 | tf_op jit(solution)/shard_map/reduce_scatter | solution.py:114
  1385.0 42.5 %reduce-scatter.18.cloned.1.call-done = bf16[256,512]{1,0:T(8,128)(2,1)} async-done(((bf16[2048,512]{1,0:T(8,128)(2,1)}), bf16[256,512]{1,0:T(8,128)(2,1)}) %reduce-scatter.18.cloned.1.call-update) | async-done | bytes 262160 | tf_op jit(solution)/shard_map/reduce_scatter | solution.py:114
  1429.3 292.3 %all-reduce.6.cloned.1.call-done = (bf16[1024,2048]{1,0:T(8,128)(2,1)}, bf16[1024,2048]{1,0:T(8,128)(2,1)}) async-done(((bf16[1024,2048]{1,0:T(8,128)(2,1)}, bf16[1024,2048]{1,0:T(8,128)(2,1)}), (bf16[1024,2048]{1,0:T(8,128)(2,1)}, bf16[1024,2048]{1,0:T(8,128)(2,1)})) %all-reduce.6.cloned.1.call-update) | async-done | bytes 8388624 | tf_op jit(solution)/shard_map/psum | solution.py:182
  (306 shorter events, 397.3 us)
Async XLA Ops:
  7.2 33.8 %all-gather.15.cloned.1.call-start = ((), (), s32[]{:S(2)}) async-start(), calls=%async_computation.10 | async-start | bytes 2359296 | tf_op jit(solution)/shard_map/all_gather | solution.py:142
  9.0 62.2 %all-gather.19.cloned.1.call-start = ((), (), s32[]{:S(2)}) async-start(), calls=%async_computation.12 | async-start | bytes 2359296 | tf_op jit(solution)/shard_map/all_gather | solution.py:143
  10.9 90.7 %all-gather.13.cloned.1.call-start = ((), (), s32[]{:S(2)}) async-start(), calls=%async_computation.9 | async-start | bytes 2359296 | tf_op jit(solution)/shard_map/all_gather | solution.py:141
  12.7 115.8 %all-gather.17.cloned.1.call-start = ((), (), s32[]{:S(2)}) async-start(), calls=%async_computation.11 | async-start | bytes 3145728 | tf_op jit(solution)/shard_map/all_gather | solution.py:163
  18.0 56.2 %copy-start.38 = (f32[1024]{0:T(1024)}, f32[1024]{0:T(1024)S(1)}, u32[]{:S(2)}) copy-start(f32[1024]{0:T(1024)S(1)} %broadcast_multiply_fusion.7) | copy-start | bytes 12292
  19.3 54.9 %copy-start.42 = (f32[1024]{0:T(1024)}, f32[1024]{0:T(1024)S(1)}, u32[]{:S(2)}) copy-start(f32[1024]{0:T(1024)S(1)} %add_rsqrt_fusion.1) | copy-start | bytes 12292
  48.1 83.5 %all-gather.29.cloned.1.call-start = ((), (), s32[]{:S(2)}) async-start(), calls=%async_computation.27 | async-start | bytes 3145728 | tf_op jit(solution)/shard_map/all_gather | solution.py:164
  79.9 86.7 %all-gather.21.cloned.1.call-start = ((), (), s32[]{:S(2)}) async-start(), calls=%async_computation.13 | async-start | bytes 2359296 | tf_op jit(solution)/shard_map/all_gather | solution.py:144
  80.7 247.7 %all-reduce.4.cloned.1.call-start = ((), (), s32[]{:S(2)}) async-start(), calls=%async_computation.14 | async-start | bytes 8388608 | tf_op jit(solution)/shard_map/psum | solution.py:174
  172.9 211.2 %all-gather.23.cloned.1.call-start = ((), (), s32[]{:S(2)}) async-start(), calls=%async_computation.15 | async-start | bytes 9437184 | tf_op jit(solution)/shard_map/all_gather | solution.py:147
  175.7 265.2 %all-gather.25.cloned.1.call-start = ((), (), s32[]{:S(2)}) async-start(), calls=%async_computation.16 | async-start | bytes 9437184 | tf_op jit(solution)/shard_map/all_gather | solution.py:148
  178.5 320.6 %all-gather.27.cloned.1.call-start = ((), (), s32[]{:S(2)}) async-start(), calls=%async_computation.17 | async-start | bytes 9437184 | tf_op jit(solution)/shard_map/all_gather | solution.py:149
  181.6 653.5 %all-gather.31.cloned.1.call-start = ((), (), s32[]{:S(2)}) async-start(), calls=%async_computation.28 | async-start | bytes 20971520 | tf_op jit(solution)/shard_map/all_gather | solution.py:203
  182.3 673.5 %copy-start.44 = (f32[1024]{0:T(1024)}, f32[1024]{0:T(1024)S(1)}, u32[]{:S(2)}) copy-start(f32[1024]{0:T(1024)S(1)} %fusion.106) | copy-start | bytes 12292
  548.2 513.6 %reduce-scatter.10.cloned.1.call-start = ((), (), s32[]{:S(2)}) async-start(), calls=%async_computation.18 | async-start | bytes 6291456 | tf_op jit(solution)/shard_map/reduce_scatter | solution.py:229
  998.8 73.1 %reduce-scatter.12.cloned.1.call-start = ((), (), s32[]{:S(2)}) async-start(), calls=%async_computation.19 | async-start | bytes 6291456 | tf_op jit(solution)/shard_map/reduce_scatter | solution.py:230
  999.6 110.5 %reduce-scatter.22.cloned.1.call-start = ((), (), s32[]{:S(2)}) async-start(), calls=%async_computation.24 | async-start | bytes 9437184 | tf_op jit(solution)/shard_map/reduce_scatter | solution.py:114
  1013.7 161.8 %reduce-scatter.24.cloned.1.call-start = ((), (), s32[]{:S(2)}) async-start(), calls=%async_computation.25 | async-start | bytes 9437184 | tf_op jit(solution)/shard_map/reduce_scatter | solution.py:114
  1027.8 222.3 %reduce-scatter.26.cloned.1.call-start = ((), (), s32[]{:S(2)}) async-start(), calls=%async_computation.26 | async-start | bytes 9437184 | tf_op jit(solution)/shard_map/reduce_scatter | solution.py:114
  1043.2 251.2 %reduce-scatter.14.cloned.1.call-start = ((), (), s32[]{:S(2)}) async-start(), calls=%async_computation.20 | async-start | bytes 2359296 | tf_op jit(solution)/shard_map/reduce_scatter | solution.py:114
  1054.2 284.5 %reduce-scatter.20.cloned.1.call-start = ((), (), s32[]{:S(2)}) async-start(), calls=%async_computation.23 | async-start | bytes 2359296 | tf_op jit(solution)/shard_map/reduce_scatter | solution.py:114
  1061.8 321.4 %reduce-scatter.16.cloned.1.call-start = ((), (), s32[]{:S(2)}) async-start(), calls=%async_computation.21 | async-start | bytes 2359296 | tf_op jit(solution)/shard_map/reduce_scatter | solution.py:114
  1070.7 356.8 %reduce-scatter.18.cloned.1.call-start = ((), (), s32[]{:S(2)}) async-start(), calls=%async_computation.22 | async-start | bytes 2359296 | tf_op jit(solution)/shard_map/reduce_scatter | solution.py:114
  1081.4 640.2 %all-reduce.6.cloned.1.call-start = ((), (), s32[]{:S(2)}) async-start(), calls=%async_computation.29 | async-start | bytes 16777216 | tf_op jit(solution)/shard_map/psum | solution.py:182
  (60 other events, 399.2 us)
Sparse Core Ops, SparseCore 0:
  10.4 30.4 all-gather.14
  43.4 27.7 all-gather.18
  73.7 27.7 all-gather.12
  103.5 10.5 all-gather.16
  115.5 11.7 all-gather.28
  129.0 29.2 all-gather.20
  173.0 155.3 all-reduce.3
  330.8 53.2 all-gather.22
  386.6 54.2 all-gather.24
  443.2 55.8 all-gather.26
  548.3 286.7 all-gather.30
  998.9 10.0 reduce-scatter.9
  1011.3 13.1 reduce-scatter.11
  1027.9 72.7 reduce-scatter.21
  1104.0 71.4 reduce-scatter.23
  1178.8 71.2 reduce-scatter.25
  1253.3 41.1 reduce-scatter.13
  1297.6 41.1 reduce-scatter.19
  1342.0 41.1 reduce-scatter.15
  1386.3 41.1 reduce-scatter.17
  1430.6 290.8 all-reduce.5
